TPU v7x, 32 devices: a whole 2x2x4 slice. The times are simulated.
32 devices in a mesh: expert: 2 (over x), dp: 16 (over z, y, core).
Axes of the slice: x: 2, y: 2, z: 4, core: 2. Of those that a mesh axis runs over, the one named last changes fastest.
Arguments:
- tokens: bfloat16 [256, 4096], P(('expert', 'dp')), may hold values from -6 to 6
- expert_ids: int32 [256, 2], P(('expert', 'dp')), may hold values from 0 to 1, as said below
- slots: int32 [256, 2], P(('expert', 'dp')), may hold values from -1 to 1, as said below
- mix_weights: float32 [256, 2], P(('expert', 'dp')), may hold values from 0.1 to 1
- w_gate: bfloat16 [2, 4096, 8192], P('expert', None, 'dp'), may hold values from -0.09375 to 0.09375
- w_up: bfloat16 [2, 4096, 8192], P('expert', None, 'dp'), may hold values from -0.09375 to 0.09375
- w_down: bfloat16 [2, 8192, 4096], P('expert', None, 'dp'), may hold values from -0.0625 to 0.0625
Outputs:
- mixed: bfloat16 [256, 4096], P(('expert', 'dp'))
Inputs may be any that keep to these rules, and one draw needn't show every extreme that they name: `expert_ids`: each token names 2 different experts. Within each aligned block of 8 tokens (the tokens of one device), the assignments to one expert get distinct slots among 0 to 1 in some order, at most 2 of them are kept and the others get -1; an expert with 2 or more assignments in the block has all 2 slots used. No two assignments of one block share an expert and a slot. In every block some expert has all 2 slots used.
All inputs are finite; a program needn't handle non-finite values.
Results may differ from a plain program's by a relative error of at most 0.0085.
Values may be sent and summed in bfloat16 or wider, within the bound.
A program may use at most 128 MiB of HBM per device.

v0:
```python
import jax
import jax.numpy as jnp
from jax import lax
from jax.sharding import PartitionSpec as P

CAP = 2


def shards(tokens, expert_ids, slots, mix_weights, w_gate, w_up, w_down):
    tok_rows, model_width = tokens.shape
    experts = lax.axis_size("expert")
    capacity = CAP
    slot_count = experts * capacity
    slot_ids = jnp.arange(slot_count, dtype=jnp.int32)
    slot_expert = slot_ids // capacity
    slot_index = slot_ids % capacity
    matches = (expert_ids[None, :, :] == slot_expert[:, None, None]) & (
        slots[None, :, :] == slot_index[:, None, None]
    )
    occupied = jnp.any(matches, axis=2)
    dispatch_table = occupied.astype(jnp.bfloat16)
    outgoing = jnp.dot(dispatch_table, tokens, preferred_element_type=jnp.float32).astype(
        jnp.bfloat16
    )
    arrived = lax.all_to_all(outgoing, "expert", split_axis=0, concat_axis=0, tiled=True)
    gate_w = w_gate[0]
    up_w = w_up[0]
    down_w = w_down[0]
    portion = lax.all_gather(arrived, "dp", axis=0, tiled=True)
    gate_part = jnp.dot(portion, gate_w, preferred_element_type=jnp.float32)
    up_part = jnp.dot(portion, up_w, preferred_element_type=jnp.float32)
    hidden = (jax.nn.silu(gate_part) * up_part).astype(jnp.bfloat16)
    summed = jnp.dot(
        lax.all_gather(hidden, "dp", axis=1, tiled=True), down_w, preferred_element_type=jnp.float32
    )
    result = summed.astype(jnp.bfloat16)
    groups = lax.axis_size("dp")
    blocks = result.reshape(groups, experts, capacity, result.shape[1])
    blocks = lax.all_to_all(blocks, "expert", split_axis=1, concat_axis=1, tiled=True)
    blocks = lax.all_to_all(blocks, "dp", split_axis=0, concat_axis=3, tiled=True)
    returned = blocks.reshape(slot_count, model_width)
    weight_table = jnp.sum(jnp.where(matches, mix_weights[None, :, :], 0.0), axis=2)
    mixed = jnp.dot(
        weight_table.T,
        returned.astype(jnp.float32),
        precision=lax.Precision.HIGHEST,
        preferred_element_type=jnp.float32,
    )
    return mixed.astype(jnp.bfloat16)


def solution(mesh):
    placed = (
        P(("expert", "dp"), None),
        P(("expert", "dp"), None),
        P(("expert", "dp"), None),
        P(("expert", "dp"), None),
        P("expert", None, "dp"),
        P("expert", None, "dp"),
        P("expert", None, "dp"),
    )
    return jax.shard_map(
        shards, mesh=mesh, in_specs=placed, out_specs=P(("expert", "dp"), None), check_vma=False
    )
```

profile of v0, /device:TPU:0, one launch (start us, length us, event | category | flops | bytes accessed | tf_op | source)
XLA Modules:
  0.0 106.0 jit_solution(6045944678401223639)
XLA Ops:
  6.5 0.0 copy-start
  6.5 0.0 all-gather.3.cloned.1.call-start
  6.5 0.8 fusion.15
  7.4 0.0 copy-done
  7.4 0.1 convolution_convert_fusion.1
  7.6 8.0 %all_to_all.32 = bf16[2,2,4096]{2,1,0:T(2,128)(2,1)S(1)} all-to-all(bf16[2,2,4096]{2,1,0:T(2,128)(2,1)S(1)} %all_to_all.22), channel_id=1, replica_groups=mesh['expert'=2,'dp'=16] {'expert'}, dimensions={0} | all-to-all | bytes 65536 | tf_op jit(solution)/shard_map/all_to_all | solution.py:25
  15.6 23.2 %all-gather = bf16[16,4,4096]{2,1,0:T(4,128)(2,1)S(1)} all-gather(bf16[1,4,4096]{2,1,0:T(4,128)(2,1)S(1)} %reshape.36), channel_id=1, replica_groups=mesh['expert'=2,'dp'=16] {'dp'}, dimensions={0}, use_global_device_ids=true | all-gather | bytes 557056 | tf_op jit(solution)/shard_map/all_gather | solution.py:29
  38.8 0.1 reshape.37
  38.9 0.0 copy-start.1
  38.9 3.2 %fusion.4 = f32[64,512]{1,0:T(8,128)S(1)} fusion(bf16[64,4096]{1,0:T(8,128)(2,1)S(1)} %reshape.37, bf16[1,4096,512]{2,1,0:T(8,128)(2,1)} %param.11), kind=kOutput, calls=%fused_computation.6 | convolution fusion | flops 268435456 | bytes 4849664 | tf_op jit(solution)/shard_map/dot_general | solution.py:30
  42.1 0.3 copy-done.1
  42.3 0.0 copy-start.2
  42.3 1.5 %fusion.9 = bf16[64,512]{1,0:T(8,128)(2,1)} fusion(bf16[64,4096]{1,0:T(8,128)(2,1)S(1)} %reshape.37, bf16[1,4096,512]{2,1,0:T(8,128)(2,1)S(1)} %copy-done.1, f32[64,512]{1,0:T(8,128)S(1)} %fusion.4), kind=kOutput, calls=%fused_computation.9 | convolution fusion | flops 268632064 | bytes 4915200 | tf_op jit(solution)/shard_map/dot_general | solution.py:31
  43.8 0.0 all-gather.3.cloned.1.call-update
  43.8 32.9 %all-gather.3.cloned.1.call-done = bf16[64,8192]{1,0:T(8,128)(2,1)} async-done(((bf16[64,512]{1,0:T(8,128)(2,1)}), bf16[64,8192]{1,0:T(8,128)(2,1)}) %all-gather.3.cloned.1.call-update) | async-done | bytes 1048592 | tf_op jit(solution)/shard_map/all_gather | solution.py:34
  76.8 3.3 %fusion.12 = bf16[64,256]{1,0:T(8,128)(2,1)S(1)} fusion(bf16[64,8192]{1,0:T(8,128)(2,1)} %all-gather.3.cloned.1.call-done, bf16[1,8192,256]{2,1,0:T(8,128)(2,1)} %param.13), kind=kOutput, calls=%fused_computation.10 | convolution fusion | flops 268451840 | bytes 5275648 | tf_op jit(solution)/shard_map/dot_general | solution.py:33
  80.1 6.5 %all_to_all.33 = bf16[16,2,2,256]{3,2,0,1:T(2,128)(2,1)S(1)} all-to-all(bf16[16,2,2,256]{3,2,0,1:T(2,128)(2,1)S(1)} %copy.25), channel_id=1, replica_groups=mesh['expert'=2,'dp'=16] {'expert'}, dimensions={1} | all-to-all | bytes 65536 | tf_op jit(solution)/shard_map/all_to_all | solution.py:39
  86.6 0.6 copy.26
  87.2 4.3 %all-to-all-start.2 = ((bf16[16,2,2,256]{3,2,1,0:T(2,128)(2,1)}), bf16[16,2,2,256]{3,2,1,0:T(2,128)(2,1)S(1)}, u32[]{:S(2)}, u32[]{:S(2)}) async-start(bf16[16,2,2,256]{3,2,1,0:T(2,128)(2,1)} %copy.26), calls=%async_computation.2 | async-start | bytes 65536 | tf_op jit(solution)/shard_map/all_to_all | solution.py:40
  91.6 0.0 copy-done.2
  91.6 6.6 %all-to-all-done.2 = bf16[16,2,2,256]{3,2,1,0:T(2,128)(2,1)S(1)} async-done(((bf16[16,2,2,256]{3,2,1,0:T(2,128)(2,1)}), bf16[16,2,2,256]{3,2,1,0:T(2,128)(2,1)S(1)}, u32[]{:S(2)}, u32[]{:S(2)}) %all-to-all-start.2) | async-done | bytes 32800 | tf_op jit(solution)/shard_map/all_to_all | solution.py:40
  98.2 0.9 convolution_convert_fusion
  (8 shorter events, 0.1 us)
Async XLA Ops:
  6.5 0.8 copy-start
  6.5 70.2 %all-gather.3.cloned.1.call-start = ((), (), s32[]{:S(2)}) async-start(), calls=%async_computation.3 | async-start | bytes 1114112 | tf_op jit(solution)/shard_map/all_gather | solution.py:34
  38.9 3.5 %copy-start.1 = (bf16[1,4096,512]{2,1,0:T(8,128)(2,1)S(1)}, bf16[1,4096,512]{2,1,0:T(8,128)(2,1)}, u32[]{:S(2)}) copy-start(bf16[1,4096,512]{2,1,0:T(8,128)(2,1)} %param.12) | copy-start | bytes 12582916
  42.3 49.2 %copy-start.2 = (f32[8,2]{0,1:T(2,128)S(1)}, f32[8,2]{0,1:T(2,128)}, u32[]{:S(2)}) copy-start(f32[8,2]{0,1:T(2,128)} %param.10) | copy-start | bytes 196
  87.2 11.0 %all-to-all-start.2 = ((bf16[16,2,2,256]{3,2,1,0:T(2,128)(2,1)}), bf16[16,2,2,256]{3,2,1,0:T(2,128)(2,1)S(1)}, u32[]{:S(2)}, u32[]{:S(2)}) async-start(bf16[16,2,2,256]{3,2,1,0:T(2,128)(2,1)} %copy.26), calls=%async_computation.2 | async-start | bytes 65536 | tf_op jit(solution)/shard_map/all_to_all | solution.py:40
Sparse Core Ops, SparseCore 0:
  44.0 32.7 all-gather.2
where the time goes:
time: 106 us
  waiting for transfers between devices  39.5 us (37%)
  blocking collectives  37.7 us (36%)
  between operations  13.5 us (13%)
  matrix products  8.99 us (8%)
  starting transfers between devices  4.33 us (4%)
  local copies, waits for them, and re-layouts  1.17 us (1%)
    all_gather x1, waiting for transfers between devices, shards(): lax.all_gather(hidden, 'dp', axis=1, tiled=True)  32.9 us
    all_gather x1, blocking collectives, shards(): portion = lax.all_gather(arrived, 'dp', axis=0, tiled=True)  23.2 us
    all_to_all x1, blocking collectives, shards(): lax.all_to_all(outgoing, 'expert', split_axis=0, concat_axis=0, tiled=True)  7.98 us
    all_to_all x1, waiting for transfers between devices, shards(): lax.all_to_all(blocks, 'dp', split_axis=0, concat_axis=3, tiled=True)  6.61 us
    all_to_all x1, blocking collectives, shards(): lax.all_to_all(blocks, 'expert', split_axis=1, concat_axis=1, tiled=True)  6.47 us
    all_to_all x1, starting transfers between devices, shards(): lax.all_to_all(blocks, 'dp', split_axis=0, concat_axis=3, tiled=True)  4.33 us
    dot_general x1, matrix products, shards(): jnp.dot(lax.all_gather(hidden, 'dp', axis=1, tiled=True), down_w, preferr...  3.31 us
    dot_general x1, matrix products, shards(): gate_part = jnp.dot(portion, gate_w, preferred_element_type=jnp.float32)  3.18 us
  transfers between devices with their start and end apart: 2, of which 2 were waited for; matrix products, arithmetic and copies ran while one was open for 0% of the time, Pallas kernels for 0%

commit v1 on v0

--- a/solution.py
+++ b/solution.py
@@ -37,7 +37,10 @@
     groups = lax.axis_size("dp")
     blocks = result.reshape(groups, experts, capacity, result.shape[1])
     blocks = lax.all_to_all(blocks, "expert", split_axis=1, concat_axis=1, tiled=True)
-    blocks = lax.all_to_all(blocks, "dp", split_axis=0, concat_axis=3, tiled=True)
+    blocks = jnp.concatenate(
+        lax.all_to_all(jnp.stack(jnp.split(blocks, lax.axis_size("dp"), axis=0)), "dp", 0, 0),
+        axis=3,
+    )
     returned = blocks.reshape(slot_count, model_width)
     weight_table = jnp.sum(jnp.where(matches, mix_weights[None, :, :], 0.0), axis=2)
     mixed = jnp.dot(

time: 106 us -> 115 us (1.085)
  local copies, waits for them, and re-layouts: 1.17 us -> 9.83 us
    unnamed x9 -> x24, local copies, waits for them, and re-layouts: 0.45 us -> 9.17 us
where the time goes in v1:
time: 115 us
  waiting for transfers between devices  39.5 us (34%)
  blocking collectives  37.7 us (33%)
  between operations  13.5 us (12%)
  local copies, waits for them, and re-layouts  9.83 us (9%)
  matrix products  8.98 us (8%)
  starting transfers between devices  4.33 us (4%)
    all_gather x1, waiting for transfers between devices, shards(): lax.all_gather(hidden, 'dp', axis=1, tiled=True)  32.9 us
    all_gather x1, blocking collectives, shards(): portion = lax.all_gather(arrived, 'dp', axis=0, tiled=True)  23.2 us
    unnamed x24, local copies, waits for them, and re-layouts  9.17 us
    all_to_all x1, blocking collectives, shards(): lax.all_to_all(outgoing, 'expert', split_axis=0, concat_axis=0, tiled=True)  7.98 us
    all_to_all x1, waiting for transfers between devices, shards(): lax.all_to_all(jnp.stack(jnp.split(blocks, lax.axis_size('dp'), axis=0)),...  6.61 us
    all_to_all x1, blocking collectives, shards(): lax.all_to_all(blocks, 'expert', split_axis=1, concat_axis=1, tiled=True)  6.47 us
    all_to_all x1, starting transfers between devices, shards(): lax.all_to_all(jnp.stack(jnp.split(blocks, lax.axis_size('dp'), axis=0)),...  4.33 us
    dot_general x1, matrix products, shards(): jnp.dot(lax.all_gather(hidden, 'dp', axis=1, tiled=True), down_w, preferr...  3.31 us
  transfers between devices with their start and end apart: 2, of which 2 were waited for; matrix products, arithmetic and copies ran while one was open for 0% of the time, Pallas kernels for 0%

profile of v1, /device:TPU:0, one launch (start us, length us, event | category | flops | bytes accessed | tf_op | source)
XLA Modules:
  0.0 114.6 jit_solution(16671751464143794837)
XLA Ops:
  6.5 0.8 fusion.15
  7.6 8.0 %all_to_all.22 = bf16[2,2,4096]{2,1,0:T(2,128)(2,1)S(1)} all-to-all(bf16[2,2,4096]{2,1,0:T(2,128)(2,1)S(1)} %all_to_all.14), channel_id=1, replica_groups=mesh['expert'=2,'dp'=16] {'expert'}, dimensions={0} | all-to-all | bytes 65536 | tf_op jit(solution)/shard_map/all_to_all | solution.py:25
  15.6 23.2 %all-gather = bf16[16,4,4096]{2,1,0:T(4,128)(2,1)S(1)} all-gather(bf16[1,4,4096]{2,1,0:T(4,128)(2,1)S(1)} %reshape.35), channel_id=1, replica_groups=mesh['expert'=2,'dp'=16] {'dp'}, dimensions={0}, use_global_device_ids=true | all-gather | bytes 557056 | tf_op jit(solution)/shard_map/all_gather | solution.py:29
  38.9 3.2 %fusion.4 = f32[64,512]{1,0:T(8,128)S(1)} fusion(bf16[64,4096]{1,0:T(8,128)(2,1)S(1)} %reshape.36, bf16[1,4096,512]{2,1,0:T(8,128)(2,1)} %param.11), kind=kOutput, calls=%fused_computation.6 | convolution fusion | flops 268435456 | bytes 4849664 | tf_op jit(solution)/shard_map/dot_general | solution.py:30
  42.3 1.5 %fusion.9 = bf16[64,512]{1,0:T(8,128)(2,1)} fusion(bf16[64,4096]{1,0:T(8,128)(2,1)S(1)} %reshape.36, bf16[1,4096,512]{2,1,0:T(8,128)(2,1)S(1)} %copy-done.1, f32[64,512]{1,0:T(8,128)S(1)} %fusion.4), kind=kOutput, calls=%fused_computation.9 | convolution fusion | flops 268632064 | bytes 4915200 | tf_op jit(solution)/shard_map/dot_general | solution.py:31
  43.8 32.9 %all-gather.3.cloned.1.call-done = bf16[64,8192]{1,0:T(8,128)(2,1)} async-done(((bf16[64,512]{1,0:T(8,128)(2,1)}), bf16[64,8192]{1,0:T(8,128)(2,1)}) %all-gather.3.cloned.1.call-update) | async-done | bytes 1048592 | tf_op jit(solution)/shard_map/all_gather | solution.py:34
  76.8 3.3 %fusion.12 = bf16[64,256]{1,0:T(8,128)(2,1)S(1)} fusion(bf16[64,8192]{1,0:T(8,128)(2,1)} %all-gather.3.cloned.1.call-done, bf16[1,8192,256]{2,1,0:T(8,128)(2,1)} %param.13), kind=kOutput, calls=%fused_computation.10 | convolution fusion | flops 268451840 | bytes 5275648 | tf_op jit(solution)/shard_map/dot_general | solution.py:33
  80.1 6.5 %all_to_all.23 = bf16[16,2,2,256]{3,2,0,1:T(2,128)(2,1)S(1)} all-to-all(bf16[16,2,2,256]{3,2,0,1:T(2,128)(2,1)S(1)} %copy.53), channel_id=1, replica_groups=mesh['expert'=2,'dp'=16] {'expert'}, dimensions={1} | all-to-all | bytes 65536 | tf_op jit(solution)/shard_map/all_to_all | solution.py:39
  86.6 0.6 constant_dynamic-update-slice_fusion.15
  88.9 0.6 constant_dynamic-update-slice_fusion.11
  89.5 0.6 constant_dynamic-update-slice_fusion.10
  90.1 0.6 constant_dynamic-update-slice_fusion.9
  90.7 0.6 constant_dynamic-update-slice_fusion.8
  91.2 0.6 constant_dynamic-update-slice_fusion.7
  91.8 0.6 constant_dynamic-update-slice_fusion.6
  92.4 0.6 constant_dynamic-update-slice_fusion.5
  93.0 0.6 constant_dynamic-update-slice_fusion.4
  93.6 0.6 constant_dynamic-update-slice_fusion.3
  94.2 0.6 constant_dynamic-update-slice_fusion.2
  94.7 0.6 constant_dynamic-update-slice_fusion.1
  95.3 0.6 constant_dynamic-update-slice_fusion
  95.9 4.3 %all-to-all-start.2 = ((bf16[16,1,2,2,256]{4,3,2,1,0:T(2,128)(2,1)}), bf16[16,1,2,2,256]{4,3,2,1,0:T(2,128)(2,1)S(1)}, u32[]{:S(2)}, u32[]{:S(2)}) async-start(bf16[16,1,2,2,256]{4,3,2,1,0:T(2,128)(2,1)} %constant_dynamic-update-slice_fusion), calls=%async_computation.2 | async-start | bytes 65536 | tf_op jit(solution)/shard_map/all_to_all | solution.py:41
  100.3 6.6 %all-to-all-done.2 = bf16[16,1,2,2,256]{4,3,2,1,0:T(2,128)(2,1)S(1)} async-done(((bf16[16,1,2,2,256]{4,3,2,1,0:T(2,128)(2,1)}), bf16[16,1,2,2,256]{4,3,2,1,0:T(2,128)(2,1)S(1)}, u32[]{:S(2)}, u32[]{:S(2)}) %all-to-all-start.2) | async-done | bytes 32800 | tf_op jit(solution)/shard_map/all_to_all | solution.py:41
  106.9 0.9 convolution_convert_fusion
  (21 shorter events, 2.4 us)
Async XLA Ops:
  6.5 0.8 copy-start
  6.5 70.2 %all-gather.3.cloned.1.call-start = ((), (), s32[]{:S(2)}) async-start(), calls=%async_computation.3 | async-start | bytes 1114112 | tf_op jit(solution)/shard_map/all_gather | solution.py:34
  38.9 3.5 %copy-start.1 = (bf16[1,4096,512]{2,1,0:T(8,128)(2,1)S(1)}, bf16[1,4096,512]{2,1,0:T(8,128)(2,1)}, u32[]{:S(2)}) copy-start(bf16[1,4096,512]{2,1,0:T(8,128)(2,1)} %param.12) | copy-start | bytes 12582916
  42.3 57.9 %copy-start.2 = (f32[8,2]{0,1:T(2,128)S(1)}, f32[8,2]{0,1:T(2,128)}, u32[]{:S(2)}) copy-start(f32[8,2]{0,1:T(2,128)} %param.10) | copy-start | bytes 196
  95.9 11.0 %all-to-all-start.2 = ((bf16[16,1,2,2,256]{4,3,2,1,0:T(2,128)(2,1)}), bf16[16,1,2,2,256]{4,3,2,1,0:T(2,128)(2,1)S(1)}, u32[]{:S(2)}, u32[]{:S(2)}) async-start(bf16[16,1,2,2,256]{4,3,2,1,0:T(2,128)(2,1)} %constant_dynamic-update-slice_fusion), calls=%async_computation.2 | async-start | bytes 65536 | tf_op jit(solution)/shard_map/all_to_all | solution.py:41
Sparse Core Ops, SparseCore 0:
  44.0 32.7 all-gather.2
